TPU v7x, 32 devices: a whole 2x2x4 slice. The times are simulated.
32 devices in a mesh: dp: 8 (over y, x, core), tensor: 4 (over z).
Axes of the slice: x: 2, y: 2, z: 4, core: 2. Of those that a mesh axis runs over, the one named last changes fastest.
Arguments:
- resid_in: float32 [8192, 2048], P(('dp', 'tensor')), may hold values from -6 to 6
- lengths: int32 [8], P('dp'), may hold values from 256 to 1024, as said below
- qkv_weight: bfloat16 [2048, 3072], P('dp', 'tensor'), may hold values from -0.125 to 0.125
- out_weight: bfloat16 [2048, 2048], P('tensor', 'dp'), may hold values from -2 to 2
- gate_weight: bfloat16 [2048, 8192], P('dp', 'tensor'), may hold values from -0.125 to 0.125
- up_weight: bfloat16 [2048, 8192], P('dp', 'tensor'), may hold values from -0.125 to 0.125
- down_weight: bfloat16 [8192, 2048], P('tensor', 'dp'), may hold values from -0.0625 to 0.0625
- attn_gain: bfloat16 [2048], P('dp'), may hold values from 0.25 to 1.75
- mlp_gain: bfloat16 [2048], P('dp'), may hold values from 0.25 to 1.75
- query_gain: float32 [64], replicated, may hold values from 0.5 to 2
- key_gain: float32 [64], replicated, may hold values from 0.5 to 2
- out_grad: float32 [8192, 2048], P(('dp', 'tensor')), may hold values from -6 to 6
Outputs:
- block_out: float32 [8192, 2048], P(('dp', 'tensor'))
- resid_grad: float32 [8192, 2048], P(('dp', 'tensor'))
- qkv_grad: float32 [2048, 3072], P('dp', 'tensor')
- outproj_grad: float32 [2048, 2048], P('tensor', 'dp')
- gate_grad: float32 [2048, 8192], P('dp', 'tensor')
- up_grad: float32 [2048, 8192], P('dp', 'tensor')
- down_grad: float32 [8192, 2048], P('tensor', 'dp')
- attngain_grad: float32 [2048], P('dp')
- mlpgain_grad: float32 [2048], P('dp')
- querygain_grad: float32 [64], replicated
- keygain_grad: float32 [64], replicated
Inputs may be any that keep to these rules, and one draw needn't show every extreme that they name: `lengths`: some batch holds a single sequence of all 1024 slots, and some batch begins with a sequence of exactly 256 slots.
All inputs are finite; a program needn't handle non-finite values.
Results may differ from a plain program's by a relative error of at most 0.024.
Values may be sent and summed in bfloat16 or wider, within the bound.
A program may use at most 256 MiB of HBM per device.

v0:
```python
import jax
import jax.numpy as jnp
from jax import lax
from jax.sharding import PartitionSpec as P

HEADS = 32
KV_HEADS = 8
HEAD_DIM = 64
EPS = 1e-05
ROPE_BASE = 1000000.0


def inv_rms(value):
    return lax.rsqrt(jnp.mean(value * value, axis=-1, keepdims=True) + EPS)


def norm_back(grad_unit, unit, inverse):
    return inverse * (grad_unit - unit * jnp.mean(grad_unit * unit, axis=-1, keepdims=True))


def rope_tables(position, head_size):
    half = head_size // 2
    freq = ROPE_BASE ** (-(2.0 * jnp.arange(half, dtype=jnp.float32)) / head_size)
    angle = position.astype(jnp.float32)[:, None] * freq[None, :]
    return (jnp.cos(angle), jnp.sin(angle))


def widen(table, ndim):
    return table.reshape(table.shape[:1] + (1,) * (ndim - 2) + table.shape[1:])


def rotate(value, cosine, sine):
    half = value.shape[-1] // 2
    first, second = (value[..., :half], value[..., half:])
    cosine, sine = (widen(cosine, value.ndim), widen(sine, value.ndim))
    return jnp.concatenate(
        [first * cosine - second * sine, second * cosine + first * sine], axis=-1
    )


def rotate_back(grad, cosine, sine):
    half = grad.shape[-1] // 2
    first, second = (grad[..., :half], grad[..., half:])
    cosine, sine = (widen(cosine, grad.ndim), widen(sine, grad.ndim))
    return jnp.concatenate(
        [first * cosine + second * sine, second * cosine - first * sine], axis=-1
    )


def visible(start, height, live):
    query_idx = start + jnp.arange(height, dtype=jnp.int32)
    key_idx = jnp.arange(live.shape[0], dtype=jnp.int32)
    query_live = lax.dynamic_slice_in_dim(live, start, height, 0)
    return (key_idx[None, :] <= query_idx[:, None]) & (query_live[:, None] == live[None, :])


def split_heads(packed_all, query_gain, key_gain, cosine, sine):
    height = packed_all.shape[0]
    group = HEADS // KV_HEADS
    packed = packed_all.reshape(height, -1, (group + 2) * HEAD_DIM)
    query = packed[:, :, : group * HEAD_DIM].reshape(height, packed.shape[1], group, HEAD_DIM)
    keys = packed[:, :, group * HEAD_DIM : (group + 1) * HEAD_DIM]
    values = packed[:, :, (group + 1) * HEAD_DIM :]
    q_inv = inv_rms(query)
    q_unit = query * q_inv
    k_inv = inv_rms(keys)
    k_unit = keys * k_inv
    q_rot = rotate(q_unit * query_gain, cosine, sine).astype(jnp.bfloat16)
    k_rot = rotate(k_unit * key_gain, cosine, sine).astype(jnp.bfloat16)
    return (q_rot, k_rot, values.astype(jnp.bfloat16), q_unit, k_unit, q_inv, k_inv)


def attend_forward(q_rot, k_rot, v_b, live):
    height = q_rot.shape[0]
    block = min(512, height)
    scale = HEAD_DIM ** (-0.5)

    def one_block(start):
        q_part = lax.dynamic_slice_in_dim(q_rot, start, block, 0)
        scores = (
            jnp.einsum("qgjd,kgd->gjqk", q_part, k_rot, preferred_element_type=jnp.float32) * scale
        )
        scores = jnp.where(visible(start, block, live), scores, -jnp.inf)
        top = jnp.max(scores, axis=-1, keepdims=True)
        expo = jnp.exp(scores - top)
        total = jnp.sum(expo, axis=-1, keepdims=True)
        probs_b = (expo / total).astype(jnp.bfloat16)
        out = jnp.einsum("gjqk,kgd->qgjd", probs_b, v_b, preferred_element_type=jnp.float32)
        return (out.astype(jnp.bfloat16), (top + jnp.log(total))[..., 0])

    starts = jnp.arange(height // block, dtype=jnp.int32) * block
    out_blocks, lse_blocks = lax.map(one_block, starts)
    return (out_blocks.reshape(q_rot.shape), lse_blocks, starts)


def attend_backward(q_rot, k_rot, v_b, live, lse_blocks, starts, grad_attn):
    height = q_rot.shape[0]
    block = min(512, height)
    scale = HEAD_DIM ** (-0.5)

    def one_block(carry, item):
        k_acc, v_acc = carry
        start, lse_part = item
        q_part = lax.dynamic_slice_in_dim(q_rot, start, block, 0)
        g_part = lax.dynamic_slice_in_dim(grad_attn, start, block, 0)
        scores = (
            jnp.einsum("qgjd,kgd->gjqk", q_part, k_rot, preferred_element_type=jnp.float32) * scale
        )
        scores = jnp.where(visible(start, block, live), scores, -jnp.inf)
        probs = jnp.exp(scores - lse_part[..., None])
        d_probs = jnp.einsum("qgjd,kgd->gjqk", g_part, v_b, preferred_element_type=jnp.float32)
        delta = jnp.sum(probs * d_probs, axis=-1, keepdims=True)
        d_scores = (probs * (d_probs - delta)).astype(jnp.bfloat16)
        probs_b = probs.astype(jnp.bfloat16)
        q_grad = (
            jnp.einsum("gjqk,kgd->qgjd", d_scores, k_rot, preferred_element_type=jnp.float32)
            * scale
        )
        k_acc = (
            k_acc
            + jnp.einsum("gjqk,qgjd->kgd", d_scores, q_part, preferred_element_type=jnp.float32)
            * scale
        )
        v_acc = v_acc + jnp.einsum(
            "gjqk,qgjd->kgd", probs_b, g_part, preferred_element_type=jnp.float32
        )
        return ((k_acc, v_acc), q_grad)

    zeros = jnp.zeros(k_rot.shape, jnp.float32)
    (k_grad, v_grad), q_blocks = lax.scan(one_block, (zeros, zeros), (starts, lse_blocks))
    return (q_blocks.reshape(q_rot.shape), k_grad, v_grad)


def merge_back(
    q_grad, k_grad, v_grad, q_unit, k_unit, q_inv, k_inv, query_gain, key_gain, cosine, sine
):
    q_turn = rotate_back(q_grad, cosine, sine)
    k_turn = rotate_back(k_grad, cosine, sine)
    qgain_part = jnp.sum(q_turn * q_unit, axis=(0, 1, 2))
    kgain_part = jnp.sum(k_turn * k_unit, axis=(0, 1))
    q_pre = norm_back(q_turn * query_gain, q_unit, q_inv)
    k_pre = norm_back(k_turn * key_gain, k_unit, k_inv)
    height = q_pre.shape[0]
    packed = jnp.concatenate([q_pre.reshape(height, q_pre.shape[1], -1), k_pre, v_grad], axis=2)
    return (packed.reshape(height, -1).astype(jnp.bfloat16), qgain_part, kgain_part)


def per_device(
    resid_in,
    lengths,
    qkv_weight,
    out_weight,
    gate_weight,
    up_weight,
    down_weight,
    attn_gain,
    mlp_gain,
    query_gain,
    key_gain,
    out_grad,
):
    f32 = jnp.float32
    bf16 = jnp.bfloat16
    tok_rows = resid_in.shape[0]
    group_rows = tok_rows * lax.axis_size("tensor")
    seq_length = lengths[0]
    slots = jnp.arange(group_rows, dtype=jnp.int32)
    live = slots < seq_length
    cosine, sine = rope_tables(jnp.where(live, slots, slots - seq_length), HEAD_DIM)
    qkv_full, out_full, gain_a = (
        lax.all_gather(qkv_weight, "dp", axis=0, tiled=True),
        lax.all_gather(out_weight, "dp", axis=1, tiled=True),
        lax.all_gather(attn_gain, "dp", axis=0, tiled=True),
    )
    inv_a = inv_rms(resid_in)
    unit_a = resid_in * inv_a
    normed_a = (unit_a * gain_a.astype(f32)).astype(bf16)
    normed_a_all = lax.all_gather(normed_a, "tensor", axis=0, tiled=True)
    packed = jnp.dot(normed_a_all, qkv_full, preferred_element_type=f32)
    q_rot, k_rot, v_b, q_unit, k_unit, q_inv, k_inv = split_heads(
        packed, query_gain, key_gain, cosine, sine
    )
    attn_out, lse_blocks, starts = attend_forward(q_rot, k_rot, v_b, live)
    attn_flat = attn_out.reshape(group_rows, -1)
    middle = resid_in + lax.psum_scatter(
        jnp.dot(attn_flat, out_full, preferred_element_type=f32).astype(jnp.bfloat16),
        "tensor",
        scatter_dimension=0,
        tiled=True,
    ).astype(jnp.float32)
    gate_full, up_full, down_full, gain_m = (
        lax.all_gather(gate_weight, "dp", axis=0, tiled=True),
        lax.all_gather(up_weight, "dp", axis=0, tiled=True),
        lax.all_gather(down_weight, "dp", axis=1, tiled=True),
        lax.all_gather(mlp_gain, "dp", axis=0, tiled=True),
    )
    inv_m = inv_rms(middle)
    unit_m = middle * inv_m
    normed_m = (unit_m * gain_m.astype(f32)).astype(bf16)
    normed_m_all = lax.all_gather(normed_m, "tensor", axis=0, tiled=True)
    gate = jnp.dot(normed_m_all, gate_full, preferred_element_type=f32)
    upper = jnp.dot(normed_m_all, up_full, preferred_element_type=f32)
    sigma = jax.nn.sigmoid(gate)
    active = gate * sigma
    hidden = (active * upper).astype(bf16)
    block_out = middle + lax.psum_scatter(
        jnp.dot(hidden, down_full, preferred_element_type=f32).astype(jnp.bfloat16),
        "tensor",
        scatter_dimension=0,
        tiled=True,
    ).astype(jnp.float32)
    gate_back, up_back, down_back, gain_mb = (
        lax.all_gather(gate_weight, "dp", axis=0, tiled=True),
        lax.all_gather(up_weight, "dp", axis=0, tiled=True),
        lax.all_gather(down_weight, "dp", axis=1, tiled=True),
        lax.all_gather(mlp_gain, "dp", axis=0, tiled=True),
    )
    grad_all = lax.all_gather(out_grad.astype(bf16), "tensor", axis=0, tiled=True)
    d_down = jnp.dot(hidden.T, grad_all, preferred_element_type=f32)
    d_hidden = jnp.dot(grad_all, down_back.T, preferred_element_type=f32)
    d_gate = (d_hidden * upper * sigma * (1.0 + gate * (1.0 - sigma))).astype(bf16)
    d_up = (d_hidden * active).astype(bf16)
    d_gatew = jnp.dot(normed_m_all.T, d_gate, preferred_element_type=f32)
    d_upw = jnp.dot(normed_m_all.T, d_up, preferred_element_type=f32)
    first = jnp.dot(d_gate, gate_back.T, preferred_element_type=f32)
    d_normed_m = lax.psum_scatter(
        (first + jnp.dot(d_up, up_back.T, preferred_element_type=f32)).astype(jnp.bfloat16),
        "tensor",
        scatter_dimension=0,
        tiled=True,
    ).astype(jnp.float32)
    mgain_part = jnp.sum(d_normed_m * unit_m, axis=0)
    d_middle = out_grad + norm_back(d_normed_m * gain_mb.astype(f32), unit_m, inv_m)
    qkv_back, out_back, gain_ab = (
        lax.all_gather(qkv_weight, "dp", axis=0, tiled=True),
        lax.all_gather(out_weight, "dp", axis=1, tiled=True),
        lax.all_gather(attn_gain, "dp", axis=0, tiled=True),
    )
    middle_all = lax.all_gather(d_middle.astype(bf16), "tensor", axis=0, tiled=True)
    d_outw = jnp.dot(attn_flat.T, middle_all, preferred_element_type=f32)
    d_attn = (
        jnp.dot(middle_all, out_back.T, preferred_element_type=f32)
        .astype(bf16)
        .reshape(attn_out.shape)
    )
    q_grad, k_grad, v_grad = attend_backward(q_rot, k_rot, v_b, live, lse_blocks, starts, d_attn)
    d_packed, qgain_part, kgain_part = merge_back(
        q_grad, k_grad, v_grad, q_unit, k_unit, q_inv, k_inv, query_gain, key_gain, cosine, sine
    )
    d_qkvw = jnp.dot(normed_a_all.T, d_packed, preferred_element_type=f32)
    d_normed_a = lax.psum_scatter(
        jnp.dot(d_packed, qkv_back.T, preferred_element_type=f32).astype(jnp.bfloat16),
        "tensor",
        scatter_dimension=0,
        tiled=True,
    ).astype(jnp.float32)
    again_part = jnp.sum(d_normed_a * unit_a, axis=0)
    resid_grad = d_middle + norm_back(d_normed_a * gain_ab.astype(f32), unit_a, inv_a)
    gate_grad, up_grad, down_grad = (
        lax.psum_scatter(
            d_gatew.astype(jnp.bfloat16), "dp", scatter_dimension=0, tiled=True
        ).astype(jnp.float32),
        lax.psum_scatter(d_upw.astype(jnp.bfloat16), "dp", scatter_dimension=0, tiled=True).astype(
            jnp.float32
        ),
        lax.psum_scatter(d_down.astype(jnp.bfloat16), "dp", scatter_dimension=1, tiled=True).astype(
            jnp.float32
        ),
    )
    qkv_grad, outproj_grad = (
        lax.psum_scatter(d_qkvw.astype(jnp.bfloat16), "dp", scatter_dimension=0, tiled=True).astype(
            jnp.float32
        ),
        lax.psum_scatter(d_outw.astype(jnp.bfloat16), "dp", scatter_dimension=1, tiled=True).astype(
            jnp.float32
        ),
    )
    again_all, mgain_all, querygain_grad, keygain_grad = lax.psum(
        (again_part, mgain_part, qgain_part, kgain_part), ("dp", "tensor")
    )
    shard_width = attn_gain.shape[0]
    offset = lax.axis_index("dp") * shard_width
    attngain_grad = lax.dynamic_slice_in_dim(again_all, offset, shard_width, 0)
    mlpgain_grad = lax.dynamic_slice_in_dim(mgain_all, offset, shard_width, 0)
    return (
        block_out,
        resid_grad,
        qkv_grad,
        outproj_grad,
        gate_grad,
        up_grad,
        down_grad,
        attngain_grad,
        mlpgain_grad,
        querygain_grad,
        keygain_grad,
    )


def solution(mesh):
    placed = (
        P(("dp", "tensor"), None),
        P("dp"),
        P("dp", "tensor"),
        P("tensor", "dp"),
        P("dp", "tensor"),
        P("dp", "tensor"),
        P("tensor", "dp"),
        P("dp"),
        P("dp"),
        P(),
        P(),
        P(("dp", "tensor"), None),
    )
    return jax.shard_map(
        per_device,
        mesh=mesh,
        in_specs=placed,
        out_specs=(
            P(("dp", "tensor"), None),
            P(("dp", "tensor"), None),
            P("dp", "tensor"),
            P("tensor", "dp"),
            P("dp", "tensor"),
            P("dp", "tensor"),
            P("tensor", "dp"),
            P("dp"),
            P("dp"),
            P(),
            P(),
        ),
        check_vma=False,
    )
```

profile of v0, /device:TPU:0, one launch (start us, length us, event | category | flops | bytes accessed | tf_op | source)
XLA Modules:
  0.0 1299.0 jit_solution(11557745781513192592)
XLA Ops:
  8.6 10.4 all-gather
  26.5 18.3 %all-gather.14.cloned.1.call-done = bf16[2048,768]{1,0:T(8,128)(2,1)} async-done(((bf16[256,768]{1,0:T(8,128)(2,1)}), bf16[2048,768]{1,0:T(8,128)(2,1)}) %all-gather.14.cloned.1.call-update) | async-done | bytes 3145744 | tf_op jit(solution)/shard_map/all_gather | solution.py:171
  44.8 82.9 %all-gather.12.cloned.1.call-done = bf16[1024,2048]{1,0:T(8,128)(2,1)} async-done(((bf16[256,2048]{1,0:T(8,128)(2,1)}), bf16[1024,2048]{1,0:T(8,128)(2,1)}) %all-gather.12.cloned.1.call-update) | async-done | bytes 4194320 | tf_op jit(solution)/shard_map/all_gather | solution.py:178
  127.7 6.2 fusion.66
  136.2 45.1 %while.27 = (s32[]{:T(128)}, bf16[2,512,2,4,64]{1,4,3,2,0:T(8,128)(2,1)S(1)}, f32[2,2,4,512]{3,2,1,0:T(4,128)}, s32[2]{0:T(128)S(1)}, pred[1024]{0:T(1024)(128)(...) while((s32[]{:T(128)}, ...), condition=%wide.region_6.7_spmd, body=%wide.region_3.6_spmd.sunk | while | flops 1125904896 | bytes 54139576 | solution.py:92
  147.6 5.1 fusion.124
  164.6 5.1 fusion.124
  183.6 6.0 convolution_convert_fusion.4
  190.3 8.9 all-gather.1
  199.3 65.9 %reduce-scatter.10.cloned.1.call-done = bf16[256,2048]{1,0:T(8,128)(2,1)} async-done(((bf16[1024,2048]{1,0:T(8,128)(2,1)}), bf16[256,2048]{1,0:T(8,128)(2,1)}) %reduce-scatter.10.cloned.1.call-update) | async-done | bytes 1048592 | tf_op jit(solution)/shard_map/reduce_scatter | solution.py:185
  273.6 48.1 %all-gather.22.cloned.1.call-done = bf16[2048,2048]{1,0:T(8,128)(2,1)} async-done(((bf16[256,2048]{1,0:T(8,128)(2,1)}), bf16[2048,2048]{1,0:T(8,128)(2,1)}) %all-gather.22.cloned.1.call-update) | async-done | bytes 8388624 | tf_op jit(solution)/shard_map/all_gather | solution.py:193
  321.7 82.8 %all-gather.18.cloned.1.call-done = bf16[1024,2048]{1,0:T(8,128)(2,1)} async-done(((bf16[256,2048]{1,0:T(8,128)(2,1)}), bf16[1024,2048]{1,0:T(8,128)(2,1)}) %all-gather.18.cloned.1.call-update) | async-done | bytes 4194320 | tf_op jit(solution)/shard_map/all_gather | solution.py:200
  404.4 14.5 %fusion.68 = f32[1024,2048]{1,0:T(8,128)} fusion(bf16[1024,2048]{1,0:T(8,128)(2,1)} %all-gather.18.cloned.1.call-done, bf16[2048,2048]{1,0:T(8,128)(2,1)} %all-gather.22.cloned.1.call-done), kind=kOutput, calls=%fused_computation.143 | convolution fusion | flops 8589934592 | bytes 20971520 | tf_op jit(solution)/shard_map/dot_general | solution.py:202
  418.9 40.2 %all-gather.20.cloned.1.call-done = bf16[2048,2048]{1,0:T(8,128)(2,1)} async-done(((bf16[256,2048]{1,0:T(8,128)(2,1)}), bf16[2048,2048]{1,0:T(8,128)(2,1)}) %all-gather.20.cloned.1.call-update) | async-done | bytes 8388624 | tf_op jit(solution)/shard_map/all_gather | solution.py:192
  459.1 14.4 %fusion.67 = f32[1024,2048]{1,0:T(8,128)} fusion(bf16[1024,2048]{1,0:T(8,128)(2,1)} %all-gather.18.cloned.1.call-done, bf16[2048,2048]{1,0:T(8,128)(2,1)} %all-gather.20.cloned.1.call-done), kind=kOutput, calls=%fused_computation.142 | convolution fusion | flops 8589934592 | bytes 20971520 | tf_op jit(solution)/shard_map/dot_general | solution.py:201
  473.5 68.5 %all-gather.26.cloned.1.call-done = bf16[1024,2048]{1,0:T(8,128)(2,1)} async-done(((bf16[256,2048]{1,0:T(8,128)(2,1)}), bf16[1024,2048]{1,0:T(8,128)(2,1)}) %all-gather.26.cloned.1.call-update) | async-done | bytes 4194320 | tf_op jit(solution)/shard_map/all_gather | solution.py:218
  542.0 56.3 %all-gather.24.cloned.1.call-done = bf16[2048,2048]{1,0:T(8,128)(2,1)} async-done(((bf16[2048,256]{1,0:T(8,128)(2,1)}), bf16[2048,2048]{1,0:T(8,128)(2,1)}) %all-gather.24.cloned.1.call-update) | async-done | bytes 8388624 | tf_op jit(solution)/shard_map/all_gather | solution.py:194
  598.3 21.8 %multiply_convert_fusion = (bf16[1024,2048]{1,0:T(8,128)(2,1)}, bf16[1024,2048]{1,0:T(8,128)(2,1)}, bf16[1024,2048]{1,0:T(8,128)(2,1)}) fusion(f32[1024,2048]{1,0:T(8,128)} %fusion.67, f32[1024,2048]{1,0:T(8,128)} %fusion.68, bf16[1024,2048]{1,0:T(8,128)(2,1)} %all-gather.26.cloned.1.call-done, bf16[2048,2048]{1,0:T(8,128)(2,1)} %all-gather.24.cloned.1.call-done), kind=kOutput, calls=%fused_computation.59 | convolution fusion | flops 8621391872 | bytes 41943040 | tf_op jit(solution)/shard_map/dot_general | solution.py:220
  620.1 12.9 fusion.69
  633.0 12.9 add_convert_fusion
  646.0 76.9 %reduce-scatter.14.cloned.1.call-done = bf16[256,2048]{1,0:T(8,128)(2,1)} async-done(((bf16[1024,2048]{1,0:T(8,128)(2,1)}), bf16[256,2048]{1,0:T(8,128)(2,1)}) %reduce-scatter.14.cloned.1.call-update) | async-done | bytes 1048592 | tf_op jit(solution)/shard_map/reduce_scatter | solution.py:226
  728.0 14.4 %convolution_convert_fusion.1 = bf16[2048,2048]{1,0:T(8,128)(2,1)} fusion(bf16[1024,2048]{1,0:T(8,128)(2,1)} %all-gather.18.cloned.1.call-done, bf16[1024,2048]{1,0:T(8,128)(2,1)} %get-tuple-element.206), kind=kOutput, calls=%fused_computation.65 | convolution fusion | flops 8594128896 | bytes 16777216 | tf_op jit(solution)/shard_map/dot_general | solution.py:224
  742.6 14.1 %convolution_convert_fusion.2 = bf16[2048,2048]{1,0:T(8,128)(2,1)} fusion(bf16[1024,2048]{1,0:T(8,128)(2,1)} %all-gather.18.cloned.1.call-done, bf16[1024,2048]{1,0:T(8,128)(2,1)} %get-tuple-element.207), kind=kOutput, calls=%fused_computation.66 | convolution fusion | flops 8594128896 | bytes 16777216 | tf_op jit(solution)/shard_map/dot_general | solution.py:223
  756.7 14.3 %convolution_convert_fusion = bf16[2048,2048]{1,0:T(8,128)(2,1)} fusion(bf16[1024,2048]{1,0:T(8,128)(2,1)} %get-tuple-element.208, bf16[1024,2048]{1,0:T(8,128)(2,1)} %all-gather.26.cloned.1.call-done), kind=kOutput, calls=%fused_computation.64 | convolution fusion | flops 8594128896 | bytes 16777216 | tf_op jit(solution)/shard_map/dot_general | solution.py:219
  772.3 37.1 %all-gather.28.cloned.1.call-done = bf16[1024,2048]{1,0:T(8,128)(2,1)} async-done(((bf16[256,2048]{1,0:T(8,128)(2,1)}), bf16[1024,2048]{1,0:T(8,128)(2,1)}) %all-gather.28.cloned.1.call-update) | async-done | bytes 4194320 | tf_op jit(solution)/shard_map/all_gather | solution.py:239
  809.4 5.8 convolution_convert_fusion.7
  815.3 6.9 convolution_convert_fusion.8
  822.3 134.1 %while.28 = (s32[]{:T(128)}, f32[1024,2,64]{0,2,1:T(8,128)}, f32[1024,2,64]{0,2,1:T(8,128)}, f32[2,512,2,4,64]{1,0,4,3,2:T(2,128)}, s32[2]{0:T(128)S(1)}, /*inde...) while((s32[]{:T(128)}, f32[1024,2,64]{0,2,1:T(8,128)}, ...), condition=%wide.region_14.15_spmd.clone, body=%wide.region_12.14_spmd.clone.sunk | while | flops 2749755904 | bytes 184474528 | solution.py:130
  830.8 5.4 fusion.138
  836.1 11.3 fusion.135
  847.4 8.7 fusion.136
  862.0 6.1 fusion.139
  869.2 19.6 %dynamic_update_slice.20 = f32[2,512,2,4,64]{1,0,4,3,2:T(2,128)} dynamic-update-slice(f32[2,512,2,4,64]{1,0,4,3,2:T(2,128)} %get-tuple-element.399, f32[1,512,2,4,64]{1,0,4,3,2:T(1,128)S(1)} %copy.52, s32[]{:T(128)S(6)} %copy.69, s32[]{:T(128)} %constant.42.clone.1..sunk.1, s32[]{:T(128)} %constant.42.clone.1..sunk.1, s32[]{:T(128)} %constant.42.clone.1..sunk.1, s32[]{:T(128)} %constant.42.clone.1..sunk.1) | dynamic-update-slice | bytes 2097156 | tf_op jit(solution)/shard_map/while/body/jit(dynamic_update_index_in_dim)/dynamic_update_slice | solution.py:130
  897.1 6.5 fusion.138
  903.6 11.2 fusion.135
  914.8 8.6 fusion.136
  929.1 6.1 fusion.139
  936.3 19.7 %dynamic_update_slice.20 = f32[2,512,2,4,64]{1,0,4,3,2:T(2,128)} dynamic-update-slice(f32[2,512,2,4,64]{1,0,4,3,2:T(2,128)} %get-tuple-element.399, f32[1,512,2,4,64]{1,0,4,3,2:T(1,128)S(1)} %copy.52, s32[]{:T(128)S(6)} %copy.69, s32[]{:T(128)} %constant.42.clone.1..sunk.1, s32[]{:T(128)} %constant.42.clone.1..sunk.1, s32[]{:T(128)} %constant.42.clone.1..sunk.1, s32[]{:T(128)} %constant.42.clone.1..sunk.1) | dynamic-update-slice | bytes 2097156 | tf_op jit(solution)/shard_map/while/body/jit(dynamic_update_index_in_dim)/dynamic_update_slice | solution.py:130
  968.4 4.9 convolution_convert_fusion.6
  973.4 7.5 convolution_convert_fusion.5
  981.0 14.1 %convolution_convert_fusion.3 = bf16[1024,2048]{1,0:T(8,128)(2,1)} fusion(bf16[1024,2048]{1,0:T(8,128)(2,1)} %get-tuple-element.208, bf16[2048,2048]{1,0:T(8,128)(2,1)} %all-gather.24.cloned.1.call-done), kind=kOutput, calls=%fused_computation.67 | convolution fusion | flops 8592031744 | bytes 16777216 | tf_op jit(solution)/shard_map/dot_general | solution.py:207
  1001.1 31.2 %reduce-scatter.26.cloned.1.call-done = bf16[2048,256]{1,0:T(8,128)(2,1)} async-done(((bf16[2048,2048]{1,0:T(8,128)(2,1)}), bf16[2048,256]{1,0:T(8,128)(2,1)}) %reduce-scatter.26.cloned.1.call-update) | async-done | bytes 1048592 | tf_op jit(solution)/shard_map/reduce_scatter | solution.py:266
  1035.2 42.0 %reduce-scatter.20.cloned.1.call-done = bf16[512,256]{1,0:T(8,128)(2,1)} async-done(((bf16[512,2048]{1,0:T(8,128)(2,1)}), bf16[512,256]{1,0:T(8,128)(2,1)}) %reduce-scatter.20.cloned.1.call-update) | async-done | bytes 262160 | tf_op jit(solution)/shard_map/reduce_scatter | solution.py:274
  1079.0 47.6 %reduce-scatter.18.cloned.1.call-done = bf16[256,768]{1,0:T(8,128)(2,1)} async-done(((bf16[2048,768]{1,0:T(8,128)(2,1)}), bf16[256,768]{1,0:T(8,128)(2,1)}) %reduce-scatter.18.cloned.1.call-update) | async-done | bytes 393232 | tf_op jit(solution)/shard_map/reduce_scatter | solution.py:271
  1128.5 77.0 %reduce-scatter.16.cloned.1.call-done = bf16[256,2048]{1,0:T(8,128)(2,1)} async-done(((bf16[1024,2048]{1,0:T(8,128)(2,1)}), bf16[256,2048]{1,0:T(8,128)(2,1)}) %reduce-scatter.16.cloned.1.call-update) | async-done | bytes 1048592 | tf_op jit(solution)/shard_map/reduce_scatter | solution.py:251
  1207.5 46.4 %all-reduce = (f32[2048]{0:T(1024)S(1)}, f32[2048]{0:T(1024)S(1)}, f32[64]{0:T(128)}, f32[64]{0:T(128)}) all-reduce(f32[2048]{0:T(1024)S(1)} %get-tuple-element.158, f32[2048]{0:T(1024)S(1)} %copy-done.36, f32[64]{0:T(128)S(1)} %reduce_sum.145, f32[64]{0:T(128)S(1)} %get-tuple-element.156), channel_id=1, replica_groups=mesh['dp'=8,'tensor'=4] {'dp','tensor'}, use_global_device_ids=true, to_apply=%region_25.26 | all-reduce | flops 4224 | bytes 33792 | tf_op jit(solution)/shard_map/psum | solution.py:278
  1255.2 30.8 %reduce-scatter.12.cloned.1.call-done = bf16[256,2048]{1,0:T(8,128)(2,1)} async-done(((bf16[1024,2048]{1,0:T(8,128)(2,1)}), bf16[256,2048]{1,0:T(8,128)(2,1)}) %reduce-scatter.12.cloned.1.call-update) | async-done | bytes 1048592 | tf_op jit(solution)/shard_map/reduce_scatter | solution.py:206
  1286.1 5.9 fusion.55
  (250 shorter events, 102.2 us)
Async XLA Ops:
  7.2 37.6 %all-gather.14.cloned.1.call-start = ((), (), s32[]{:S(2)}) async-start(), calls=%async_computation.10 | async-start | bytes 3538944 | tf_op jit(solution)/shard_map/all_gather | solution.py:171
  7.9 119.8 %all-gather.12.cloned.1.call-start = ((), (), s32[]{:S(2)}) async-start(), calls=%async_computation.9 | async-start | bytes 5242880 | tf_op jit(solution)/shard_map/all_gather | solution.py:178
  24.4 158.3 %all-gather.16.cloned.1.call-start = ((), (), s32[]{:S(2)}) async-start(), calls=%async_computation.11 | async-start | bytes 2359296 | tf_op jit(solution)/shard_map/all_gather | solution.py:172
  25.1 240.0 %reduce-scatter.10.cloned.1.call-start = ((), (), s32[]{:S(2)}) async-start(), calls=%async_computation.12 | async-start | bytes 5242880 | tf_op jit(solution)/shard_map/reduce_scatter | solution.py:185
  26.5 109.3 %copy-start.20 = (f32[1024,32]{0,1:T(8,128)}, f32[1024,32]{0,1:T(8,128)S(1)}, u32[]{:S(2)}) copy-start(f32[1024,32]{0,1:T(8,128)S(1)} %get-tuple-element.223) | copy-start | bytes 393220
  26.5 109.3 %copy-start.22 = (f32[1024,32]{0,1:T(8,128)}, f32[1024,32]{0,1:T(8,128)S(1)}, u32[]{:S(2)}) copy-start(f32[1024,32]{0,1:T(8,128)S(1)} %get-tuple-element.224) | copy-start | bytes 393220
  26.5 107.9 %copy-start.43 = (f32[64]{0:T(128)S(1)}, f32[64]{0:T(128)}, u32[]{:S(2)}) copy-start(f32[64]{0:T(128)} %param.26) | copy-start | bytes 772
  181.3 8.4 copy-start.34
  181.3 8.3 copy-start.51
  189.6 75.5 %copy-start.1 = (f32[256,2048]{1,0:T(8,128)S(1)}, f32[256,2048]{1,0:T(8,128)}, u32[]{:S(2)}) copy-start(f32[256,2048]{1,0:T(8,128)} %param.16) | copy-start | bytes 6291460
  189.7 132.0 %all-gather.22.cloned.1.call-start = ((), (), s32[]{:S(2)}) async-start(), calls=%async_computation.15 | async-start | bytes 9437184 | tf_op jit(solution)/shard_map/all_gather | solution.py:193
  190.3 214.2 %all-gather.18.cloned.1.call-start = ((), (), s32[]{:S(2)}) async-start(), calls=%async_computation.13 | async-start | bytes 5242880 | tf_op jit(solution)/shard_map/all_gather | solution.py:200
  199.2 526.5 %copy-start.28 = (f32[8,1,256]{2,1,0:T(1,128)}, f32[8,1,256]{2,1,0:T(1,128)S(1)}, u32[]{:S(2)}) copy-start(f32[8,1,256]{2,1,0:T(1,128)S(1)} %convert_element_type.146) | copy-start | bytes 24580
  266.7 459.0 %copy-start.37 = (f32[256]{0:T(256)}, f32[256]{0:T(256)S(1)}, u32[]{:S(2)}) copy-start(f32[256]{0:T(256)S(1)} %add_rsqrt_fusion.2) | copy-start | bytes 3076
  269.3 189.8 %all-gather.20.cloned.1.call-start = ((), (), s32[]{:S(2)}) async-start(), calls=%async_computation.14 | async-start | bytes 9437184 | tf_op jit(solution)/shard_map/all_gather | solution.py:192
  270.0 272.0 %all-gather.26.cloned.1.call-start = ((), (), s32[]{:S(2)}) async-start(), calls=%async_computation.18 | async-start | bytes 5242880 | tf_op jit(solution)/shard_map/all_gather | solution.py:218
  272.8 325.5 %all-gather.24.cloned.1.call-start = ((), (), s32[]{:S(2)}) async-start(), calls=%async_computation.16 | async-start | bytes 9437184 | tf_op jit(solution)/shard_map/all_gather | solution.py:194
  273.5 449.3 %reduce-scatter.14.cloned.1.call-start = ((), (), s32[]{:S(2)}) async-start(), calls=%async_computation.19 | async-start | bytes 5242880 | tf_op jit(solution)/shard_map/reduce_scatter | solution.py:226
  620.1 12.9 copy-start.53
  645.9 77.0 %copy-start.12 = (bf16[256,2048]{1,0:T(8,128)(2,1)S(1)}, bf16[256,2048]{1,0:T(8,128)(2,1)}, u32[]{:S(2)}) copy-start(bf16[256,2048]{1,0:T(8,128)(2,1)} %reduce-scatter.10.cloned.1.call-done) | copy-start | bytes 3145732
  645.9 163.5 %all-gather.28.cloned.1.call-start = ((), (), s32[]{:S(2)}) async-start(), calls=%async_computation.20 | async-start | bytes 5242880 | tf_op jit(solution)/shard_map/all_gather | solution.py:239
  728.0 267.1 %reduce-scatter.24.cloned.1.call-start = ((), (), s32[]{:S(2)}) async-start(), calls=%async_computation.25 | async-start | bytes 9437184 | tf_op jit(solution)/shard_map/reduce_scatter | solution.py:263
  742.5 255.6 %reduce-scatter.22.cloned.1.call-start = ((), (), s32[]{:S(2)}) async-start(), calls=%async_computation.24 | async-start | bytes 9437184 | tf_op jit(solution)/shard_map/reduce_scatter | solution.py:260
  756.7 275.7 %reduce-scatter.26.cloned.1.call-start = ((), (), s32[]{:S(2)}) async-start(), calls=%async_computation.26 | async-start | bytes 9437184 | tf_op jit(solution)/shard_map/reduce_scatter | solution.py:266
  771.0 38.4 %copy-start.25 = (bf16[64,8,2,512]{3,1,2,0:T(8,128)(2,1)S(1)}, bf16[64,8,2,512]{3,1,2,0:T(8,128)(2,1)}, u32[]{:S(2)}) copy-start(bf16[64,8,2,512]{3,1,2,0:T(8,128)(2,1)} %copy-done.24) | copy-start | bytes 3145732
  771.0 306.2 %reduce-scatter.20.cloned.1.call-start = ((), (), s32[]{:S(2)}) async-start(), calls=%async_computation.23 | async-start | bytes 2359296 | tf_op jit(solution)/shard_map/reduce_scatter | solution.py:274
  815.3 7.0 copy-start.6
  815.3 7.0 copy-start.16
  815.3 7.0 copy-start.35
  815.3 7.0 copy-start.52
  815.3 311.2 %reduce-scatter.18.cloned.1.call-start = ((), (), s32[]{:S(2)}) async-start(), calls=%async_computation.22 | async-start | bytes 3538944 | tf_op jit(solution)/shard_map/reduce_scatter | solution.py:271
  847.4 12.0 copy-start.4
  847.4 12.0 copy-start.7
  914.8 11.8 copy-start.4
  914.8 11.8 copy-start.7
  956.4 7.2 copy-start.11
  956.4 7.2 copy-start.27
  956.4 7.2 copy-start.47
  973.3 232.2 %reduce-scatter.16.cloned.1.call-start = ((), (), s32[]{:S(2)}) async-start(), calls=%async_computation.21 | async-start | bytes 5242880 | tf_op jit(solution)/shard_map/reduce_scatter | solution.py:251
  981.0 305.1 %reduce-scatter.12.cloned.1.call-start = ((), (), s32[]{:S(2)}) async-start(), calls=%async_computation.17 | async-start | bytes 5242880 | tf_op jit(solution)/shard_map/reduce_scatter | solution.py:206
  998.1 207.5 %copy-start.2 = (f32[256,2048]{1,0:T(8,128)S(1)}, f32[256,2048]{1,0:T(8,128)}, u32[]{:S(2)}) copy-start(f32[256,2048]{1,0:T(8,128)} %param.16) | copy-start | bytes 6291460
  998.1 207.5 %copy-start.33 = (f32[8,1,256]{2,1,0:T(1,128)S(1)}, f32[8,1,256]{2,1,0:T(1,128)}, u32[]{:S(2)}) copy-start(f32[8,1,256]{2,1,0:T(1,128)} %copy-done.32) | copy-start | bytes 24580
  998.1 207.5 %copy-start.40 = (f32[256]{0:T(256)S(1)}, f32[256]{0:T(256)}, u32[]{:S(2)}) copy-start(f32[256]{0:T(256)} %copy-done.39) | copy-start | bytes 3076
  1001.1 206.4 %copy-start.36 = (f32[2048]{0:T(1024)S(1)}, f32[2048]{0:T(1024)}, u32[]{:S(2)}) copy-start(f32[2048]{0:T(1024)} %get-tuple-element.154) | copy-start | bytes 24580
  1001.1 284.9 %copy-start.13 = (bf16[256,2048]{1,0:T(8,128)(2,1)S(1)}, bf16[256,2048]{1,0:T(8,128)(2,1)}, u32[]{:S(2)}) copy-start(bf16[256,2048]{1,0:T(8,128)(2,1)} %reduce-scatter.10.cloned.1.call-done) | copy-start | bytes 3145732
  1001.1 284.9 %copy-start.29 = (f32[8,1,256]{2,1,0:T(1,128)S(1)}, f32[8,1,256]{2,1,0:T(1,128)}, u32[]{:S(2)}) copy-start(f32[8,1,256]{2,1,0:T(1,128)} %copy-done.28) | copy-start | bytes 24580
  1001.1 284.9 %copy-start.38 = (f32[256]{0:T(256)S(1)}, f32[256]{0:T(256)}, u32[]{:S(2)}) copy-start(f32[256]{0:T(256)} %copy-done.37) | copy-start | bytes 3076
  1001.1 284.9 %copy-start.42 = (f32[256]{0:T(256)S(1)}, f32[256]{0:T(256)}, u32[]{:S(2)}) copy-start(f32[256]{0:T(256)} %copy-done.41) | copy-start | bytes 3076
  (30 other events, 64.0 us)
Sparse Core Ops, SparseCore 0:
  9.9 34.8 all-gather.13
  46.9 80.7 all-gather.11
  129.6 26.5 all-gather.15
  189.8 75.2 reduce-scatter.9
  266.9 54.7 all-gather.21
  323.7 80.7 all-gather.17
  406.3 52.7 all-gather.19
  461.2 80.7 all-gather.25
  543.9 54.3 all-gather.23
  646.0 76.7 reduce-scatter.13
  728.1 81.2 all-gather.27
  812.7 69.9 reduce-scatter.23
  886.2 71.4 reduce-scatter.21
  961.0 71.3 reduce-scatter.25
  1036.1 41.0 reduce-scatter.19
  1080.4 46.0 reduce-scatter.17
  1128.7 76.7 reduce-scatter.15
  1207.7 78.3 reduce-scatter.11
where the time goes:
time: 1310 us; the launch traced here: 1300 us
  waiting for transfers between devices  809 us (62%)
  matrix products  245 us (19%)
  other arithmetic  75.4 us (6%)
  local copies, waits for them, and re-layouts  67.6 us (5%)
  blocking collectives  65.7 us (5%)
  loops' own time  19.6 us (1%)
  between operations  15.9 us (1%)
    all_gather x1, waiting for transfers between devices, per_device(): normed_a_all = lax.all_gather(normed_a, 'tensor', axis=0, tiled=True)  82.9 us
    all_gather x1, waiting for transfers between devices, per_device(): normed_m_all = lax.all_gather(normed_m, 'tensor', axis=0, tiled=True)  82.8 us
    reduce_scatter x1, waiting for transfers between devices, per_device(): lax.psum_scatter(jnp.dot(d_packed, qkv_back.T, preferred_element_type=f32...  77 us
    reduce_scatter x1, waiting for transfers between devices, per_device(): lax.psum_scatter((first + jnp.dot(d_up, up_back.T, preferred_element_type...  76.9 us
    all_gather x1, waiting for transfers between devices, per_device(): lax.all_gather(out_grad.astype(bf16), 'tensor', axis=0, tiled=True)  68.5 us
    reduce_scatter x1, waiting for transfers between devices, per_device(): lax.psum_scatter(jnp.dot(attn_flat, out_full, preferred_element_type=f32)...  65.9 us
    all_gather x1, waiting for transfers between devices, per_device(): lax.all_gather(down_weight, 'dp', axis=1, tiled=True)  56.3 us
    all_gather x1, waiting for transfers between devices, per_device(): lax.all_gather(up_weight, 'dp', axis=0, tiled=True)  48.1 us
  transfers between devices with their start and end apart: 18, of which 15 were waited for; matrix products, arithmetic and copies ran while one was open for 24% of the time, Pallas kernels for 0%

commit v1 on v0

--- a/solution.py
+++ b/solution.py
@@ -197,7 +197,14 @@
     inv_m = inv_rms(middle)
     unit_m = middle * inv_m
     normed_m = (unit_m * gain_m.astype(f32)).astype(bf16)
-    normed_m_all = lax.all_gather(normed_m, "tensor", axis=0, tiled=True)
+    ring = [normed_m]
+    for hop in range(3):
+        ring.append(lax.ppermute(ring[-1], "tensor", [(dev, (dev + 1) % 4) for dev in range(4)]))
+    normed_m_all = jnp.roll(
+        jnp.concatenate(ring[::-1], axis=0),
+        (lax.axis_index("tensor") + 1) * ring[0].shape[0],
+        axis=0,
+    )
     gate = jnp.dot(normed_m_all, gate_full, preferred_element_type=f32)
     upper = jnp.dot(normed_m_all, up_full, preferred_element_type=f32)
     sigma = jax.nn.sigmoid(gate)

time: 1310 us -> 1270 us (0.969)
  waiting for transfers between devices: 809 us -> 718 us
  starting transfers between devices: 0.73 us -> 32.2 us
  local copies, waits for them, and re-layouts: 67.6 us -> 82.7 us
    ppermute x0 -> x3, waiting for transfers between devices: none -> 84.4 us  [per_device(): lax.ppermute(ring[-1], 'tensor', [(dev, (dev + 1) % 4) for dev in range(4)])]
    all_gather x1 -> x0, waiting for transfers between devices: 82.8 us -> none  [per_device(): normed_m_all = lax.all_gather(normed_m, 'tensor', axis=0, tiled=True)]
    all_gather x1, waiting for transfers between devices: 68.5 us -> 0.99 us  [per_device(): lax.all_gather(out_grad.astype(bf16), 'tensor', axis=0, tiled=True)]
    ppermute x0 -> x3, starting transfers between devices: none -> 31.5 us  [per_device(): lax.ppermute(ring[-1], 'tensor', [(dev, (dev + 1) % 4) for dev in range(4)])]
    all_gather x1, waiting for transfers between devices: 48.1 us -> 25.5 us  [per_device(): lax.all_gather(up_weight, 'dp', axis=0, tiled=True)]
    unnamed x99 -> x108, local copies, waits for them, and re-layouts: 6.55 us -> 20.6 us
  transfers between devices with their start and end apart: 18 -> 20, of which waited for: 15 -> 16; matrix products, arithmetic and copies ran while one was open for 24% -> 26% of each run, Pallas kernels for 0% -> 0%
where the time goes in v1:
time: 1270 us; the launch traced here: 1250 us
  waiting for transfers between devices  718 us (57%)
  matrix products  256 us (20%)
  local copies, waits for them, and re-layouts  82.7 us (7%)
  other arithmetic  74.6 us (6%)
  blocking collectives  65.7 us (5%)
  starting transfers between devices  32.2 us (3%)
  between operations  15.8 us (1%)
    ppermute x3, waiting for transfers between devices, per_device(): lax.ppermute(ring[-1], 'tensor', [(dev, (dev + 1) % 4) for dev in range(4)])  84.4 us
    all_gather x1, waiting for transfers between devices, per_device(): normed_a_all = lax.all_gather(normed_a, 'tensor', axis=0, tiled=True)  82.9 us
    reduce_scatter x1, waiting for transfers between devices, per_device(): lax.psum_scatter(jnp.dot(d_packed, qkv_back.T, preferred_element_type=f32...  77.1 us
    reduce_scatter x1, waiting for transfers between devices, per_device(): lax.psum_scatter((first + jnp.dot(d_up, up_back.T, preferred_element_type...  76.9 us
    reduce_scatter x1, waiting for transfers between devices, per_device(): lax.psum_scatter(jnp.dot(attn_flat, out_full, preferred_element_type=f32)...  61.4 us
    all_gather x1, waiting for transfers between devices, per_device(): lax.all_gather(down_weight, 'dp', axis=1, tiled=True)  55.8 us
    reduce_scatter x1, waiting for transfers between devices, per_device(): lax.psum_scatter(d_qkvw.astype(jnp.bfloat16), 'dp', scatter_dimension=0,...  47.5 us
    psum x1, blocking collectives, per_device(): lax.psum((again_part, mgain_part, qgain_part, kgain_part), ('dp', 'tensor'))  46.4 us
  transfers between devices with their start and end apart: 20, of which 16 were waited for; matrix products, arithmetic and copies ran while one was open for 26% of the time, Pallas kernels for 0%

profile of v1, /device:TPU:0, one launch (start us, length us, event | category | flops | bytes accessed | tf_op | source)
XLA Modules:
  0.0 1253.1 jit_solution(13652743929578401874)
XLA Ops:
  8.6 10.4 all-gather
  26.4 18.4 %all-gather.13.cloned.1.call-done = bf16[2048,768]{1,0:T(8,128)(2,1)} async-done(((bf16[256,768]{1,0:T(8,128)(2,1)}), bf16[2048,768]{1,0:T(8,128)(2,1)}) %all-gather.13.cloned.1.call-update) | async-done | bytes 3145744 | tf_op jit(solution)/shard_map/all_gather | solution.py:171
  44.8 82.9 %all-gather.11.cloned.1.call-done = bf16[1024,2048]{1,0:T(8,128)(2,1)} async-done(((bf16[256,2048]{1,0:T(8,128)(2,1)}), bf16[1024,2048]{1,0:T(8,128)(2,1)}) %all-gather.11.cloned.1.call-update) | async-done | bytes 4194320 | tf_op jit(solution)/shard_map/all_gather | solution.py:178
  127.7 6.2 fusion.76
  136.2 34.3 %while.27 = (s32[]{:T(128)}, bf16[2,512,2,4,64]{1,4,3,2,0:T(8,128)(2,1)S(1)}, f32[2,2,4,512]{3,2,1,0:T(4,128)}, s32[2]{0:T(128)S(1)}, pred[1024]{0:T(1024)(128)(...) while((s32[]{:T(128)}, ...), condition=%wide.region_6.7_spmd, body=%wide.region_3.6_spmd.sunk | while | flops 1125904896 | bytes 54139576 | solution.py:92
  164.6 5.1 fusion.129
  172.0 6.4 convolution_convert_fusion.4
  183.5 8.9 all-gather.1
  192.4 61.4 %reduce-scatter.10.cloned.1.call-done = bf16[256,2048]{1,0:T(8,128)(2,1)} async-done(((bf16[1024,2048]{1,0:T(8,128)(2,1)}), bf16[256,2048]{1,0:T(8,128)(2,1)}) %reduce-scatter.10.cloned.1.call-update) | async-done | bytes 1048592 | tf_op jit(solution)/shard_map/reduce_scatter | solution.py:185
  258.6 40.7 %collective-permute-done = bf16[256,2048]{1,0:T(8,128)(2,1)} collective-permute-done((bf16[256,2048]{1,0:T(8,128)(2,1)S(1)}, bf16[256,2048]{1,0:T(8,128)(2,1)}, u32[]{:S(2)}, u32[]{:S(2)}) %collective-permute-start) | collective-permute-done | bytes 1048608 | tf_op jit(solution)/shard_map/ppermute | solution.py:202
  299.3 18.5 %collective-permute-start.1 = (bf16[256,2048]{1,0:T(8,128)(2,1)}, bf16[256,2048]{1,0:T(8,128)(2,1)}, u32[]{:S(2)}, u32[]{:S(2)}) collective-permute-start(bf16[256,2048]{1,0:T(8,128)(2,1)} %collective-permute-done), channel_id=1, source_target_pairs={{0,1},{1,2},{2,3},{3,0},{4,5},{5,6},{6,7},{7,4},{8,9},{9,10},{10,1... | collective-permute-start | bytes 3145736 | tf_op jit(solution)/shard_map/ppermute | solution.py:202
  317.8 43.6 %collective-permute-done.1 = bf16[256,2048]{1,0:T(8,128)(2,1)} collective-permute-done((bf16[256,2048]{1,0:T(8,128)(2,1)}, bf16[256,2048]{1,0:T(8,128)(2,1)}, u32[]{:S(2)}, u32[]{:S(2)}) %collective-permute-start.1) | collective-permute-done | bytes 1048608 | tf_op jit(solution)/shard_map/ppermute | solution.py:202
  361.5 11.5 collective-permute-start.2
  373.9 55.8 %all-gather.21.cloned.1.call-done = bf16[2048,2048]{1,0:T(8,128)(2,1)} async-done(((bf16[2048,256]{1,0:T(8,128)(2,1)}), bf16[2048,2048]{1,0:T(8,128)(2,1)}) %all-gather.21.cloned.1.call-update) | async-done | bytes 8388624 | tf_op jit(solution)/shard_map/all_gather | solution.py:194
  429.8 14.6 %fusion.77 = f32[1024,2048]{1,0:T(8,128)} fusion(bf16[1024,2048]{1,0:T(8,128)(2,1)} %all-gather.23.cloned.1.call-done, bf16[2048,2048]{1,0:T(8,128)(2,1)} %all-gather.21.cloned.1.call-done), kind=kOutput, calls=%fused_computation.160 | convolution fusion | flops 8589934592 | bytes 20971520 | tf_op jit(solution)/shard_map/dot_general | solution.py:227
  460.5 25.5 %all-gather.19.cloned.1.call-done = bf16[2048,2048]{1,0:T(8,128)(2,1)} async-done(((bf16[256,2048]{1,0:T(8,128)(2,1)}), bf16[2048,2048]{1,0:T(8,128)(2,1)}) %all-gather.19.cloned.1.call-update) | async-done | bytes 8388624 | tf_op jit(solution)/shard_map/all_gather | solution.py:193
  485.9 14.5 %fusion.51 = f32[1024,2048]{1,0:T(8,128)} fusion(bf16[2048,2048]{1,0:T(8,128)(2,1)} %all-gather.19.cloned.1.call-done, bf16[2048,2048]{1,0:T(8,128)(2,1)} %constant_dynamic-update-slice_fusion, s32[]{:T(128)S(6)} %select_n.49), kind=kOutput, calls=%fused_computation.76 | convolution fusion | flops 8589934592 | bytes 20971524 | tf_op jit(solution)/shard_map/dot_general | solution.py:209
  500.5 41.6 %all-gather.17.cloned.1.call-done = bf16[2048,2048]{1,0:T(8,128)(2,1)} async-done(((bf16[256,2048]{1,0:T(8,128)(2,1)}), bf16[2048,2048]{1,0:T(8,128)(2,1)}) %all-gather.17.cloned.1.call-update) | async-done | bytes 8388624 | tf_op jit(solution)/shard_map/all_gather | solution.py:192
  542.1 22.5 %multiply_convert_fusion = (bf16[1024,2048]{1,0:T(8,128)(2,1)}, bf16[1024,2048]{1,0:T(8,128)(2,1)}, bf16[1024,2048]{1,0:T(8,128)(2,1)}) fusion(f32[1024,2048]{1,0:T(8,128)} %fusion.77, f32[1024,2048]{1,0:T(8,128)} %fusion.51, bf16[2048,2048]{1,0:T(8,128)(2,1)} %all-gather.17.cloned.1.call-done, bf16[2048,2048]{1,0:T(8,128)(2,1)} %constant_dynamic-update-slice_fusion, ...), kind=kOutput, calls=%fused_computation.59 | convolution fusion | flops 8621391872 | bytes 41943044 | tf_op jit(solution)/shard_map/dot_general | solution.py:208
  564.6 23.3 %fusion.78 = f32[1024,2048]{1,0:T(8,128)} fusion(bf16[1024,2048]{1,0:T(8,128)(2,1)} %get-tuple-element.207, bf16[2048,2048]{1,0:T(8,128)(2,1)} %all-gather.17.cloned.1.call-done), kind=kOutput, calls=%fused_computation.161 | convolution fusion | flops 8589934592 | bytes 20971520 | tf_op jit(solution)/shard_map/dot_general | solution.py:232
  587.9 12.2 add_convert_fusion
  600.1 76.9 %reduce-scatter.14.cloned.1.call-done = bf16[256,2048]{1,0:T(8,128)(2,1)} async-done(((bf16[1024,2048]{1,0:T(8,128)(2,1)}), bf16[256,2048]{1,0:T(8,128)(2,1)}) %reduce-scatter.14.cloned.1.call-update) | async-done | bytes 1048592 | tf_op jit(solution)/shard_map/reduce_scatter | solution.py:233
  682.2 14.0 %convolution_convert_fusion.1 = bf16[2048,2048]{1,0:T(8,128)(2,1)} fusion(bf16[1024,2048]{1,0:T(8,128)(2,1)} %get-tuple-element.206, bf16[2048,2048]{1,0:T(8,128)(2,1)} %constant_dynamic-update-slice_fusion, s32[]{:T(128)S(6)} %select_n.49), kind=kOutput, calls=%fused_computation.65 | convolution fusion | flops 8594128896 | bytes 16777220 | tf_op jit(solution)/shard_map/dot_general | solution.py:231
  696.2 14.4 %convolution_convert_fusion.2 = bf16[2048,2048]{1,0:T(8,128)(2,1)} fusion(bf16[1024,2048]{1,0:T(8,128)(2,1)} %get-tuple-element.207, bf16[2048,2048]{1,0:T(8,128)(2,1)} %constant_dynamic-update-slice_fusion, s32[]{:T(128)S(6)} %select_n.49), kind=kOutput, calls=%fused_computation.66 | convolution fusion | flops 8594128896 | bytes 16777220 | tf_op jit(solution)/shard_map/dot_general | solution.py:230
  710.7 14.0 %convolution_convert_fusion = bf16[2048,2048]{1,0:T(8,128)(2,1)} fusion(bf16[1024,2048]{1,0:T(8,128)(2,1)} %get-tuple-element.208, bf16[1024,2048]{1,0:T(8,128)(2,1)} %all-gather.23.cloned.1.call-done), kind=kOutput, calls=%fused_computation.64 | convolution fusion | flops 8594128896 | bytes 16777216 | tf_op jit(solution)/shard_map/dot_general | solution.py:226
  726.1 37.4 %all-gather.25.cloned.1.call-done = bf16[1024,2048]{1,0:T(8,128)(2,1)} async-done(((bf16[256,2048]{1,0:T(8,128)(2,1)}), bf16[1024,2048]{1,0:T(8,128)(2,1)}) %all-gather.25.cloned.1.call-update) | async-done | bytes 4194320 | tf_op jit(solution)/shard_map/all_gather | solution.py:246
  763.5 5.8 convolution_convert_fusion.7
  769.5 6.9 convolution_convert_fusion.8
  776.4 133.9 %while.28 = (s32[]{:T(128)}, f32[1024,2,64]{0,2,1:T(8,128)}, f32[1024,2,64]{0,2,1:T(8,128)}, f32[2,512,2,4,64]{1,0,4,3,2:T(2,128)}, s32[2]{0:T(128)S(1)}, /*inde...) while((s32[]{:T(128)}, f32[1024,2,64]{0,2,1:T(8,128)}, ...), condition=%wide.region_14.15_spmd.clone, body=%wide.region_12.14_spmd.clone.sunk | while | flops 2749755904 | bytes 184474528 | solution.py:130
  784.9 5.4 fusion.143
  790.2 11.3 fusion.140
  801.5 8.8 fusion.141
  816.1 6.1 fusion.144
  823.3 19.6 %dynamic_update_slice.20 = f32[2,512,2,4,64]{1,0,4,3,2:T(2,128)} dynamic-update-slice(f32[2,512,2,4,64]{1,0,4,3,2:T(2,128)} %get-tuple-element.399, f32[1,512,2,4,64]{1,0,4,3,2:T(1,128)S(1)} %copy.52, s32[]{:T(128)S(6)} %copy.76, s32[]{:T(128)} %constant.57.clone.1..sunk.1, s32[]{:T(128)} %constant.57.clone.1..sunk.1, s32[]{:T(128)} %constant.57.clone.1..sunk.1, s32[]{:T(128)} %constant.57.clone.1..sunk.1) | dynamic-update-slice | bytes 2097156 | tf_op jit(solution)/shard_map/while/body/jit(dynamic_update_index_in_dim)/dynamic_update_slice | solution.py:130
  851.2 6.5 fusion.143
  857.7 11.2 fusion.140
  868.9 8.6 fusion.141
  883.3 6.1 fusion.144
  890.5 19.7 %dynamic_update_slice.20 = f32[2,512,2,4,64]{1,0,4,3,2:T(2,128)} dynamic-update-slice(f32[2,512,2,4,64]{1,0,4,3,2:T(2,128)} %get-tuple-element.399, f32[1,512,2,4,64]{1,0,4,3,2:T(1,128)S(1)} %copy.52, s32[]{:T(128)S(6)} %copy.76, s32[]{:T(128)} %constant.57.clone.1..sunk.1, s32[]{:T(128)} %constant.57.clone.1..sunk.1, s32[]{:T(128)} %constant.57.clone.1..sunk.1, s32[]{:T(128)} %constant.57.clone.1..sunk.1) | dynamic-update-slice | bytes 2097156 | tf_op jit(solution)/shard_map/while/body/jit(dynamic_update_index_in_dim)/dynamic_update_slice | solution.py:130
  927.4 7.6 convolution_convert_fusion.5
  935.1 14.1 %convolution_convert_fusion.3 = bf16[1024,2048]{1,0:T(8,128)(2,1)} fusion(bf16[1024,2048]{1,0:T(8,128)(2,1)} %get-tuple-element.208, bf16[2048,2048]{1,0:T(8,128)(2,1)} %all-gather.21.cloned.1.call-done), kind=kOutput, calls=%fused_computation.67 | convolution fusion | flops 8592031744 | bytes 16777216 | tf_op jit(solution)/shard_map/dot_general | solution.py:214
  955.3 31.3 %reduce-scatter.26.cloned.1.call-done = bf16[2048,256]{1,0:T(8,128)(2,1)} async-done(((bf16[2048,2048]{1,0:T(8,128)(2,1)}), bf16[2048,256]{1,0:T(8,128)(2,1)}) %reduce-scatter.26.cloned.1.call-update) | async-done | bytes 1048592 | tf_op jit(solution)/shard_map/reduce_scatter | solution.py:273
  989.4 42.1 %reduce-scatter.20.cloned.1.call-done = bf16[512,256]{1,0:T(8,128)(2,1)} async-done(((bf16[512,2048]{1,0:T(8,128)(2,1)}), bf16[512,256]{1,0:T(8,128)(2,1)}) %reduce-scatter.20.cloned.1.call-update) | async-done | bytes 262160 | tf_op jit(solution)/shard_map/reduce_scatter | solution.py:281
  1033.3 47.5 %reduce-scatter.18.cloned.1.call-done = bf16[256,768]{1,0:T(8,128)(2,1)} async-done(((bf16[2048,768]{1,0:T(8,128)(2,1)}), bf16[256,768]{1,0:T(8,128)(2,1)}) %reduce-scatter.18.cloned.1.call-update) | async-done | bytes 393232 | tf_op jit(solution)/shard_map/reduce_scatter | solution.py:278
  1082.7 77.1 %reduce-scatter.16.cloned.1.call-done = bf16[256,2048]{1,0:T(8,128)(2,1)} async-done(((bf16[1024,2048]{1,0:T(8,128)(2,1)}), bf16[256,2048]{1,0:T(8,128)(2,1)}) %reduce-scatter.16.cloned.1.call-update) | async-done | bytes 1048592 | tf_op jit(solution)/shard_map/reduce_scatter | solution.py:258
  1161.8 46.4 %all-reduce = (f32[2048]{0:T(1024)S(1)}, f32[2048]{0:T(1024)S(1)}, f32[64]{0:T(128)}, f32[64]{0:T(128)}) all-reduce(f32[2048]{0:T(1024)S(1)} %get-tuple-element.158, f32[2048]{0:T(1024)S(1)} %copy-done.36, f32[64]{0:T(128)S(1)} %reduce_sum.145, f32[64]{0:T(128)S(1)} %get-tuple-element.156), channel_id=1, replica_groups=mesh['dp'=8,'tensor'=4] {'dp','tensor'}, use_global_device_ids=true, to_apply=%region_25.26 | all-reduce | flops 4224 | bytes 33792 | tf_op jit(solution)/shard_map/psum | solution.py:285
  1209.5 30.8 %reduce-scatter.12.cloned.1.call-done = bf16[256,2048]{1,0:T(8,128)(2,1)} async-done(((bf16[1024,2048]{1,0:T(8,128)(2,1)}), bf16[256,2048]{1,0:T(8,128)(2,1)}) %reduce-scatter.12.cloned.1.call-update) | async-done | bytes 1048592 | tf_op jit(solution)/shard_map/reduce_scatter | solution.py:213
  1240.3 5.9 fusion.61
  (263 shorter events, 129.0 us)
Async XLA Ops:
  7.2 37.6 %all-gather.13.cloned.1.call-start = ((), (), s32[]{:S(2)}) async-start(), calls=%async_computation.10 | async-start | bytes 3538944 | tf_op jit(solution)/shard_map/all_gather | solution.py:171
  7.9 119.8 %all-gather.11.cloned.1.call-start = ((), (), s32[]{:S(2)}) async-start(), calls=%async_computation.9 | async-start | bytes 5242880 | tf_op jit(solution)/shard_map/all_gather | solution.py:178
  24.3 147.6 %all-gather.15.cloned.1.call-start = ((), (), s32[]{:S(2)}) async-start(), calls=%async_computation.11 | async-start | bytes 2359296 | tf_op jit(solution)/shard_map/all_gather | solution.py:172
  25.1 228.8 %reduce-scatter.10.cloned.1.call-start = ((), (), s32[]{:S(2)}) async-start(), calls=%async_computation.12 | async-start | bytes 5242880 | tf_op jit(solution)/shard_map/reduce_scatter | solution.py:185
  26.4 109.3 %copy-start.20 = (f32[1024,32]{0,1:T(8,128)}, f32[1024,32]{0,1:T(8,128)S(1)}, u32[]{:S(2)}) copy-start(f32[1024,32]{0,1:T(8,128)S(1)} %get-tuple-element.223) | copy-start | bytes 393220
  26.4 109.3 %copy-start.22 = (f32[1024,32]{0,1:T(8,128)}, f32[1024,32]{0,1:T(8,128)S(1)}, u32[]{:S(2)}) copy-start(f32[1024,32]{0,1:T(8,128)S(1)} %get-tuple-element.224) | copy-start | bytes 393220
  26.4 108.0 %copy-start.43 = (f32[64]{0:T(128)S(1)}, f32[64]{0:T(128)}, u32[]{:S(2)}) copy-start(f32[64]{0:T(128)} %param.26) | copy-start | bytes 772
  170.5 7.8 copy-start.3
  170.5 7.8 copy-start.5
  170.6 7.8 copy-start.15
  170.6 7.8 copy-start.34
  170.6 7.8 copy-start.52
  178.4 75.4 %copy-start.1 = (f32[256,2048]{1,0:T(8,128)S(1)}, f32[256,2048]{1,0:T(8,128)}, u32[]{:S(2)}) copy-start(f32[256,2048]{1,0:T(8,128)} %param.16) | copy-start | bytes 6291460
  178.5 195.5 %all-gather.23.cloned.1.call-start = ((), (), s32[]{:S(2)}) async-start(), calls=%async_computation.17 | async-start | bytes 5242880 | tf_op jit(solution)/shard_map/all_gather | solution.py:225
  181.4 248.4 %all-gather.21.cloned.1.call-start = ((), (), s32[]{:S(2)}) async-start(), calls=%async_computation.15 | async-start | bytes 9437184 | tf_op jit(solution)/shard_map/all_gather | solution.py:194
  182.0 304.0 %all-gather.19.cloned.1.call-start = ((), (), s32[]{:S(2)}) async-start(), calls=%async_computation.14 | async-start | bytes 9437184 | tf_op jit(solution)/shard_map/all_gather | solution.py:193
  182.7 359.4 %all-gather.17.cloned.1.call-start = ((), (), s32[]{:S(2)}) async-start(), calls=%async_computation.13 | async-start | bytes 9437184 | tf_op jit(solution)/shard_map/all_gather | solution.py:192
  183.5 493.6 %reduce-scatter.14.cloned.1.call-start = ((), (), s32[]{:S(2)}) async-start(), calls=%async_computation.18 | async-start | bytes 5242880 | tf_op jit(solution)/shard_map/reduce_scatter | solution.py:233
  192.4 487.5 %copy-start.28 = (f32[8,1,256]{2,1,0:T(1,128)}, f32[8,1,256]{2,1,0:T(1,128)S(1)}, u32[]{:S(2)}) copy-start(f32[8,1,256]{2,1,0:T(1,128)S(1)} %convert_element_type.146) | copy-start | bytes 24580
  255.5 424.4 %copy-start.37 = (f32[256]{0:T(256)}, f32[256]{0:T(256)S(1)}, u32[]{:S(2)}) copy-start(f32[256]{0:T(256)S(1)} %add_rsqrt_fusion.2) | copy-start | bytes 3076
  257.0 42.3 %collective-permute-start = (bf16[256,2048]{1,0:T(8,128)(2,1)S(1)}, bf16[256,2048]{1,0:T(8,128)(2,1)}, u32[]{:S(2)}, u32[]{:S(2)}) collective-permute-start(bf16[256,2048]{1,0:T(8,128)(2,1)S(1)} %multiply_convert_fusion.3), channel_id=1, source_target_pairs={{0,1},{1,2},{2,3},{3,0},{4,5},{5,6},{6,7},{7,4},{8,9},{9,10},{10,1... | collective-permute-start | bytes 3145736 | tf_op jit(solution)/shard_map/ppermute | solution.py:202
  299.3 62.2 %collective-permute-start.1 = (bf16[256,2048]{1,0:T(8,128)(2,1)}, bf16[256,2048]{1,0:T(8,128)(2,1)}, u32[]{:S(2)}, u32[]{:S(2)}) collective-permute-start(bf16[256,2048]{1,0:T(8,128)(2,1)} %collective-permute-done), channel_id=1, source_target_pairs={{0,1},{1,2},{2,3},{3,0},{4,5},{5,6},{6,7},{7,4},{8,9},{9,10},{10,1... | collective-permute-start | bytes 3145736 | tf_op jit(solution)/shard_map/ppermute | solution.py:202
  361.5 82.9 %collective-permute-start.2 = (bf16[256,2048]{1,0:T(8,128)(2,1)}, bf16[256,2048]{1,0:T(8,128)(2,1)}, u32[]{:S(2)}, u32[]{:S(2)}) collective-permute-start(bf16[256,2048]{1,0:T(8,128)(2,1)} %collective-permute-done.1), channel_id=1, source_target_pairs={{0,1},{1,2},{2,3},{3,0},{4,5},{5,6},{6,7},{7,4},{8,9},{9,10},{10,1... | collective-permute-start | bytes 3145736 | tf_op jit(solution)/shard_map/ppermute | solution.py:202
  564.6 23.3 %copy-start.49 = (bf16[2048,2048]{1,0:T(8,128)(2,1)S(1)}, bf16[2048,2048]{1,0:T(8,128)(2,1)}, u32[]{:S(2)}) copy-start(bf16[2048,2048]{1,0:T(8,128)(2,1)} %all-gather.19.cloned.1.call-done) | copy-start | bytes 25165828
  564.6 23.3 %copy-start.54 = (bf16[1024,2048]{1,0:T(8,128)(2,1)S(1)}, bf16[1024,2048]{1,0:T(8,128)(2,1)}, u32[]{:S(2)}) copy-start(bf16[1024,2048]{1,0:T(8,128)(2,1)} %get-tuple-element.206) | copy-start | bytes 12582916
  600.1 77.0 %copy-start.12 = (bf16[256,2048]{1,0:T(8,128)(2,1)S(1)}, bf16[256,2048]{1,0:T(8,128)(2,1)}, u32[]{:S(2)}) copy-start(bf16[256,2048]{1,0:T(8,128)(2,1)} %reduce-scatter.10.cloned.1.call-done) | copy-start | bytes 3145732
  600.1 163.4 %all-gather.25.cloned.1.call-start = ((), (), s32[]{:S(2)}) async-start(), calls=%async_computation.19 | async-start | bytes 5242880 | tf_op jit(solution)/shard_map/all_gather | solution.py:246
  682.1 267.1 %reduce-scatter.24.cloned.1.call-start = ((), (), s32[]{:S(2)}) async-start(), calls=%async_computation.24 | async-start | bytes 9437184 | tf_op jit(solution)/shard_map/reduce_scatter | solution.py:270
  696.2 256.0 %reduce-scatter.22.cloned.1.call-start = ((), (), s32[]{:S(2)}) async-start(), calls=%async_computation.23 | async-start | bytes 9437184 | tf_op jit(solution)/shard_map/reduce_scatter | solution.py:267
  710.7 275.9 %reduce-scatter.26.cloned.1.call-start = ((), (), s32[]{:S(2)}) async-start(), calls=%async_computation.25 | async-start | bytes 9437184 | tf_op jit(solution)/shard_map/reduce_scatter | solution.py:273
  724.8 38.7 %copy-start.25 = (bf16[64,8,2,512]{3,1,2,0:T(8,128)(2,1)S(1)}, bf16[64,8,2,512]{3,1,2,0:T(8,128)(2,1)}, u32[]{:S(2)}) copy-start(bf16[64,8,2,512]{3,1,2,0:T(8,128)(2,1)} %copy-done.24) | copy-start | bytes 3145732
  724.8 306.7 %reduce-scatter.20.cloned.1.call-start = ((), (), s32[]{:S(2)}) async-start(), calls=%async_computation.22 | async-start | bytes 2359296 | tf_op jit(solution)/shard_map/reduce_scatter | solution.py:281
  769.4 311.4 %reduce-scatter.18.cloned.1.call-start = ((), (), s32[]{:S(2)}) async-start(), calls=%async_computation.21 | async-start | bytes 3538944 | tf_op jit(solution)/shard_map/reduce_scatter | solution.py:278
  801.5 12.1 copy-start.4
  801.5 12.1 copy-start.7
  868.9 11.9 copy-start.4
  868.9 11.9 copy-start.7
  910.3 7.2 copy-start.11
  927.4 232.4 %reduce-scatter.16.cloned.1.call-start = ((), (), s32[]{:S(2)}) async-start(), calls=%async_computation.20 | async-start | bytes 5242880 | tf_op jit(solution)/shard_map/reduce_scatter | solution.py:258
  935.1 305.2 %reduce-scatter.12.cloned.1.call-start = ((), (), s32[]{:S(2)}) async-start(), calls=%async_computation.16 | async-start | bytes 5242880 | tf_op jit(solution)/shard_map/reduce_scatter | solution.py:213
  952.2 207.6 %copy-start.2 = (f32[256,2048]{1,0:T(8,128)S(1)}, f32[256,2048]{1,0:T(8,128)}, u32[]{:S(2)}) copy-start(f32[256,2048]{1,0:T(8,128)} %param.16) | copy-start | bytes 6291460
  952.2 207.6 %copy-start.33 = (f32[8,1,256]{2,1,0:T(1,128)S(1)}, f32[8,1,256]{2,1,0:T(1,128)}, u32[]{:S(2)}) copy-start(f32[8,1,256]{2,1,0:T(1,128)} %copy-done.32) | copy-start | bytes 24580
  952.2 207.6 %copy-start.40 = (f32[256]{0:T(256)S(1)}, f32[256]{0:T(256)}, u32[]{:S(2)}) copy-start(f32[256]{0:T(256)} %copy-done.39) | copy-start | bytes 3076
  955.3 206.5 %copy-start.36 = (f32[2048]{0:T(1024)S(1)}, f32[2048]{0:T(1024)}, u32[]{:S(2)}) copy-start(f32[2048]{0:T(1024)} %get-tuple-element.154) | copy-start | bytes 24580
  955.3 285.0 %copy-start.13 = (bf16[256,2048]{1,0:T(8,128)(2,1)S(1)}, bf16[256,2048]{1,0:T(8,128)(2,1)}, u32[]{:S(2)}) copy-start(bf16[256,2048]{1,0:T(8,128)(2,1)} %reduce-scatter.10.cloned.1.call-done) | copy-start | bytes 3145732
  955.3 285.0 %copy-start.29 = (f32[8,1,256]{2,1,0:T(1,128)S(1)}, f32[8,1,256]{2,1,0:T(1,128)}, u32[]{:S(2)}) copy-start(f32[8,1,256]{2,1,0:T(1,128)} %copy-done.28) | copy-start | bytes 24580
  955.3 285.0 %copy-start.38 = (f32[256]{0:T(256)S(1)}, f32[256]{0:T(256)}, u32[]{:S(2)}) copy-start(f32[256]{0:T(256)} %copy-done.37) | copy-start | bytes 3076
  955.3 285.0 %copy-start.42 = (f32[256]{0:T(256)S(1)}, f32[256]{0:T(256)}, u32[]{:S(2)}) copy-start(f32[256]{0:T(256)} %copy-done.41) | copy-start | bytes 3076
  (33 other events, 111.9 us)
Sparse Core Ops, SparseCore 0:
  9.9 34.8 all-gather.12
  46.9 80.7 all-gather.10
  129.6 26.6 all-gather.14
  178.5 75.2 reduce-scatter.9
  255.9 118.0 all-gather.22
  375.6 54.0 all-gather.20
  431.6 54.2 all-gather.18
  487.8 54.2 all-gather.16
  600.2 76.7 reduce-scatter.13
  682.2 81.2 all-gather.24
  767.0 69.9 reduce-scatter.23
  840.3 71.4 reduce-scatter.21
  915.3 71.2 reduce-scatter.25
  990.3 41.1 reduce-scatter.19
  1034.7 46.0 reduce-scatter.17
  1082.9 76.7 reduce-scatter.15
  1161.9 78.3 reduce-scatter.11
